TPU v7x, 32 devices: a whole 2x2x4 slice. The times are simulated.
32 devices in a mesh: prompt: 4 (over y, core), seq: 4 (over z), head: 2 (over x).
Axes of the slice: x: 2, y: 2, z: 4, core: 2. Of those that a mesh axis runs over, the one named last changes fastest.
Arguments:
- queries: bfloat16 [16, 64, 1280], P(('prompt', 'seq'), None, 'head'), parts along dimension 0, may hold values from -1024 to 1024
- prefix_keys: bfloat16 [65536, 256], P(('prompt', 'seq'), 'head'), parts along dimension 0, may hold values from -6 to 6
- prefix_values: bfloat16 [65536, 256], P(('prompt', 'seq'), 'head'), parts along dimension 0, may hold values from -6 to 6
- suffix_keys: bfloat16 [16, 2048, 256], P(('prompt', 'seq'), None, 'head'), parts along dimension 0, may hold values from -6 to 6
- suffix_values: bfloat16 [16, 2048, 256], P(('prompt', 'seq'), None, 'head'), parts along dimension 0, may hold values from -6 to 6
- kept_blocks: int32 [16, 16], P('prompt'), parts along dimension 0, may hold values from 0 to 127, as said below
- suffix_lengths: int32 [16], P(('prompt', 'seq')), parts along dimension 0, may hold values from 64 to 2048, as said below
- out_weight: bfloat16 [1280, 5120], P('head', 'seq'), may hold values from -1.75 to 1.75
Outputs:
- projected: float32 [1024, 5120], P(('prompt', 'head'), 'seq'), parts along dimension 0
There are 4 independent parts, one for each index of `prompt`. A program takes and returns all parts, laid end to end along the dimension named above; an argument that names none is the same for every part. Nothing has to cross between parts.
Inputs may be any that keep to these rules, and one draw needn't show every extreme that they name: `kept_blocks`: each row names 16 different prefix blocks. Among the blocks k * 32 to (k + 1) * 32 - 1, for each k, at most 8 are named by one row, and every row names exactly 8 of one such run. `suffix_lengths`: A sample's query tokens are the last 64 of its filled slots; some sample fills all 2048.
All inputs are finite; a program needn't handle non-finite values.
Results may differ from a plain program's by a relative error of at most 0.008.
Values may be sent and summed in bfloat16 or wider, within the bound.
A program may use at most 64 MiB of HBM per device.

v0:
```python
import functools
import math

import jax
import jax.numpy as jnp
from jax import lax
from jax.experimental import pallas as pl
from jax.experimental.pallas import tpu as pltpu
from jax.sharding import PartitionSpec as P

HD = 128
GQA = 5
BLOCK = 128
MOST = 8
CHUNK = MOST * BLOCK

floor_value = -1e30
hidden_value = -3e30
factor = math.log2(math.e) / math.sqrt(HD)


def chosen_slots(kept, sample, base, blocks_here):
    slots = [jnp.int32(0)] * MOST
    count = jnp.int32(0)
    for e in range(kept.shape[1]):
        local = kept[sample, e] - base
        present = (local >= 0) & (local < blocks_here)
        rank = jnp.where(present, count, -1)
        slots = [jnp.where(rank == j, local, slots[j]) for j in range(MOST)]
        count = count + jnp.where(present, 1, 0)
    return slots, count


def rows_of(block):
    return jnp.concatenate([block[:, j * HD : (j + 1) * HD] for j in range(GQA)], axis=0)


def scores_of(asking, keys):
    return lax.dot_general(asking, keys, (((1,), (1,)), ((), ())), preferred_element_type=jnp.float32)


def softmax_part(scores, values):
    maximum = jnp.maximum(jnp.max(scores, axis=-1, keepdims=True), floor_value)
    weights = jnp.exp2((scores - maximum) * factor).astype(jnp.bfloat16)
    weight_sum = jnp.sum(weights.astype(jnp.float32), axis=-1, keepdims=True)
    return maximum, weight_sum, jnp.dot(weights, values, preferred_element_type=jnp.float32)


def kernel(
    n, heads,
    q_hbm, pk_hbm, pv_hbm, sk_hbm, sv_hbm, kept, lengths, w_hbm,
    out,
    qbuf, pk, pv, sk, sv, wall, own_acc, own_max, own_sum, psend, pbuf, ssend, sbuf, att, fbuf,
    lsem, q_s, q_r, p_s, p_r, s_s, s_r, a_s, a_r, f_s, f_r, w_s, w_r, v_s, v_r,
):
    me = lax.axis_index("seq")
    head = lax.axis_index("head")
    prompt = lax.axis_index("prompt")
    side = prompt % 2
    twin = prompt + 1 - 2 * side
    tokens = q_hbm.shape[0]
    blocks_here = pk_hbm.shape[0]
    base = me * blocks_here
    per_head = n // heads

    def partner(r):
        found, bit = 0, 1
        while bit < n:
            found = found + (me // bit + r // bit) % 2 * bit
            bit *= 2
        return found

    def turn(i):
        return (i + n // 2 - 1) % (n - 1) + 1

    loads = [
        pltpu.make_async_copy(src, dst, lsem.at[i])
        for i, (src, dst) in enumerate(
            ((q_hbm, qbuf.at[0]), (sk_hbm, sk), (sv_hbm, sv), (pk_hbm, pk), (pv_hbm, pv), (w_hbm, wall.at[head]))
        )
    ]
    for load in loads:
        load.start()

    barrier = pltpu.get_barrier_semaphore()
    for r in range(1, n):
        pl.semaphore_signal(barrier, inc=1, device_id={"seq": partner(r)})
    for r in range(1, heads):
        pl.semaphore_signal(barrier, inc=1, device_id={"head": lax.rem(head + r, heads)})
    pl.semaphore_signal(barrier, inc=1, device_id={"prompt": twin})
    pl.semaphore_wait(barrier, n - 1 + heads - 1 + 1)

    def query_copy(r):
        return pltpu.make_async_remote_copy(
            qbuf.at[0], qbuf.at[r], q_s.at[r], q_r.at[r], device_id={"seq": partner(r)}
        )

    def part_copy(r):
        return pltpu.make_async_remote_copy(
            psend.at[r], pbuf.at[r], p_s.at[r], p_r.at[r], device_id={"seq": partner(r)}
        )

    def stat_copy(r):
        return pltpu.make_async_remote_copy(
            ssend.at[r], sbuf.at[r], s_s.at[r], s_r.at[r], device_id={"seq": partner(r)}
        )

    def attended_copy(r, sample):
        return pltpu.make_async_remote_copy(
            att.at[sample], att.at[sample], a_s.at[r], a_r.at[sample], device_id={"seq": partner(r)}
        )

    def forward_copy(r, sample):
        place = lax.rem(sample, per_head)
        return pltpu.make_async_remote_copy(
            att.at[sample], fbuf.at[r, place], f_s.at[r, place], f_r.at[r, place],
            device_id={"head": lax.rem(head + r, heads)},
        )

    half = w_hbm.shape[0] // 2

    def source(r):
        return lax.rem(head + heads - r, heads)

    def weight_copy(r, owner):
        place = wall.at[owner, pl.ds(side * half, half)]
        return pltpu.make_async_remote_copy(
            place, place, w_s.at[r], w_r.at[r], device_id={"head": lax.rem(head + r, heads)}
        )

    def twin_copy(r, which):
        place = wall.at[source(r), pl.ds(which * half, half)]
        return pltpu.make_async_remote_copy(place, place, v_s.at[r], v_r.at[r], device_id={"prompt": twin})

    loads[0].wait()
    for i in range(n - 1):
        query_copy(turn(i)).start()
    loads[5].wait()
    for r in range(1, heads):
        weight_copy(r, head).start()

    def prefix_part(asking, sample):
        slots, count = chosen_slots(kept, sample, base, blocks_here)
        keys = jnp.concatenate([pk[slot] for slot in slots], axis=0)
        values = jnp.concatenate([pv[slot] for slot in slots], axis=0)
        column = lax.broadcasted_iota(jnp.int32, (1, CHUNK), 1)
        hidden = jnp.where(column < count * BLOCK, 0.0, hidden_value)
        return softmax_part(scores_of(asking, keys) + hidden, values)

    asking = rows_of(qbuf[0])
    rows = asking.shape[0]
    last_seen = lengths[0] - tokens + lax.broadcasted_iota(jnp.int32, (rows, 1), 0) % tokens
    loads[1].wait()
    loads[2].wait()

    def own_scores(keys, start):
        column = start + lax.broadcasted_iota(jnp.int32, (1, keys.shape[0]), 1)
        return jnp.where(column <= last_seen, scores_of(asking, keys), hidden_value)

    def merged(one, two):
        maximum = jnp.maximum(one[0], two[0])
        shrink_one = jnp.exp2((one[0] - maximum) * factor)
        shrink_two = jnp.exp2((two[0] - maximum) * factor)
        return (
            maximum,
            one[1] * shrink_one + two[1] * shrink_two,
            one[2] * shrink_one + two[2] * shrink_two,
        )

    state = None
    for start in range(0, sk.shape[0], CHUNK):
        piece = pl.ds(start, min(CHUNK, sk.shape[0] - start))
        latest = softmax_part(own_scores(sk[piece], start), sv[piece])
        state = latest if state is None else merged(state, latest)
    loads[3].wait()
    loads[4].wait()
    state = merged(state, prefix_part(asking, me))
    own_max[...] = jnp.broadcast_to(state[0], own_max.shape)
    own_sum[...] = jnp.broadcast_to(state[1], own_sum.shape)
    own_acc[...] = state[2]

    lane = lax.broadcasted_iota(jnp.int32, (tokens, HD), 1)

    def remote_part(i, carry):
        r = turn(i)
        query_copy(r).wait_recv()
        maximum, weight_sum, summed = prefix_part(rows_of(qbuf[r]), partner(r))
        mean = (summed / jnp.maximum(weight_sum, 1e-30)).astype(jnp.bfloat16)
        stats = jnp.zeros((tokens, HD), jnp.float32)
        for j in range(GQA):
            piece = slice(j * tokens, (j + 1) * tokens)
            psend[r, :, j * HD : (j + 1) * HD] = mean[piece]
            stats = jnp.where(lane == j, maximum[piece], stats)
            stats = jnp.where(lane == GQA + j, weight_sum[piece], stats)
        part_copy(r).start()
        square = jnp.concatenate([stats, jnp.zeros((HD - tokens, HD), jnp.float32)], axis=0)
        ssend[r] = square.T[: ssend.shape[1]]
        stat_copy(r).start()
        return carry

    lax.fori_loop(0, n - 1, remote_part, 0)

    def stats_from(r):
        part_copy(r).wait_recv()
        stat_copy(r).wait_recv()
        padded = jnp.concatenate([sbuf[r], jnp.zeros((HD - sbuf.shape[1], HD), jnp.float32)], axis=0)
        return padded.T[:tokens]

    stats = [stats_from(r) for r in range(1, n)]
    for j in range(GQA):
        piece = pl.ds(j * tokens, tokens)
        columns = slice(j * HD, (j + 1) * HD)
        maximum = own_max[piece]
        for one in stats:
            maximum = jnp.maximum(maximum, one[:, j : j + 1])
        scale = jnp.exp2((own_max[piece] - maximum) * factor)
        total = own_acc[piece] * scale
        weight_sum = own_sum[piece] * scale
        for r, one in zip(range(1, n), stats):
            share = jnp.exp2((one[:, j : j + 1] - maximum) * factor) * one[:, GQA + j : GQA + j + 1]
            total = total + share * pbuf[r, :, columns].astype(jnp.float32)
            weight_sum = weight_sum + share
        att[me, :, columns] = (total / weight_sum).astype(jnp.bfloat16)
    for i in range(n - 1):
        attended_copy(turn(i), me).start()

    def forward(sample):
        reader = sample // per_head

        @pl.when(reader != head)
        def _():
            forward_copy(lax.rem(reader + heads - head, heads), sample).start()

    forward(me)
    for r in range(1, heads):
        weight_copy(r, source(r)).wait_recv()
        twin_copy(r, side).start()
    for i in range(n - 1):
        sample = partner(turn(i))
        attended_copy(turn(i), sample).wait_recv()
        forward(sample)

    def projected(block, owner):
        return jnp.dot(
            block.reshape(per_head * tokens, block.shape[-1]), wall[owner], preferred_element_type=jnp.float32
        )

    out[...] = projected(att[pl.ds(head * per_head, per_head)], head)
    for r in range(1, heads):
        twin_copy(r, 1 - side).wait_recv()
        for i in range(per_head):
            forward_copy(r, i).wait_recv()
        out[...] += projected(fbuf[r], source(r))

    for r in range(1, n):
        query_copy(r).wait_send()
        part_copy(r).wait_send()
        stat_copy(r).wait_send()
        attended_copy(r, me).wait_send()
    for r in range(1, heads):
        weight_copy(r, head).wait_send()
        twin_copy(r, side).wait_send()
        for i in range(per_head):
            forward_copy(r, i).wait_send()


def body(n, heads, queries, prefix_keys, prefix_values, suffix_keys, suffix_values, kept_blocks, suffix_lengths, out_weight):
    tokens, width = queries.shape[1:]
    blocks_here = prefix_keys.shape[0] // BLOCK
    slots = suffix_keys.shape[1]
    columns = out_weight.shape[1]
    per_head = n // heads
    assert prefix_keys.shape[1] == HD and width == GQA * HD and n % heads == 0
    assert n & (n - 1) == 0
    bf16, f32 = jnp.bfloat16, jnp.float32
    any_space = pl.BlockSpec(memory_space=pltpu.HBM)
    smem = pl.BlockSpec(memory_space=pltpu.SMEM)
    dma = pltpu.SemaphoreType.DMA
    return pl.pallas_call(
        functools.partial(kernel, n, heads),
        out_shape=jax.ShapeDtypeStruct((per_head * tokens, columns), f32),
        in_specs=[any_space] * 5 + [smem] * 2 + [any_space],
        out_specs=pl.BlockSpec(memory_space=pltpu.VMEM),
        scratch_shapes=[
            pltpu.VMEM((n, tokens, width), bf16),
            pltpu.VMEM((blocks_here, BLOCK, HD), bf16),
            pltpu.VMEM((blocks_here, BLOCK, HD), bf16),
            pltpu.VMEM((slots, HD), bf16),
            pltpu.VMEM((slots, HD), bf16),
            pltpu.VMEM((heads,) + out_weight.shape, bf16),
            pltpu.VMEM((GQA * tokens, HD), f32),
            pltpu.VMEM((GQA * tokens, HD), f32),
            pltpu.VMEM((GQA * tokens, HD), f32),
            pltpu.VMEM((n, tokens, width), bf16),
            pltpu.VMEM((n, tokens, width), bf16),
            pltpu.VMEM((n, 16, HD), f32),
            pltpu.VMEM((n, 16, HD), f32),
            pltpu.VMEM((n, tokens, width), bf16),
            pltpu.VMEM((heads, per_head, tokens, width), bf16),
            dma((6,)),
            dma((n,)), dma((n,)),
            dma((n,)), dma((n,)),
            dma((n,)), dma((n,)),
            dma((n,)), dma((n,)),
            dma((heads, per_head)), dma((heads, per_head)),
            dma((heads,)), dma((heads,)),
            dma((heads,)), dma((heads,)),
        ],
        compiler_params=pltpu.CompilerParams(
            collective_id=0, has_side_effects=True, vmem_limit_bytes=63 * 1024 * 1024
        ),
    )(
        queries[0],
        prefix_keys.reshape(blocks_here, BLOCK, HD),
        prefix_values.reshape(blocks_here, BLOCK, HD),
        suffix_keys[0],
        suffix_values[0],
        kept_blocks,
        suffix_lengths,
        out_weight,
    )


def solution(mesh):
    in_specs = (
        P(("prompt", "seq"), None, "head"),
        P(("prompt", "seq"), "head"),
        P(("prompt", "seq"), "head"),
        P(("prompt", "seq"), None, "head"),
        P(("prompt", "seq"), None, "head"),
        P("prompt", None),
        P(("prompt", "seq")),
        P("head", "seq"),
    )
    out_specs = P(("prompt", "head"), "seq")
    part = functools.partial(body, mesh.shape["seq"], mesh.shape["head"])
    return jax.shard_map(part, mesh=mesh, in_specs=in_specs, out_specs=out_specs, check_vma=False)
```

profile of v0, /device:TPU:2, one launch (start us, length us, event | category | flops | bytes accessed | tf_op | source)
XLA Modules:
  0.0 36.2 jit_solution(7390959646201558687)
XLA Ops:
  0.7 33.6 %shard_map.82 = f32[128,1280]{1,0:T(8,128)} custom-call(bf16[64,640]{1,0:T(8,128)(2,1)} %bitcast.9, bf16[32,128,128]{2,1,0:T(8,128)(2,1)} %bitcast.5, bf16[32,128,128]{2,1,0:T(8,128)(2,1)} %bitcast.6, bf16[2048,128]{1,0:T(8,128)(2,1)} %bitcast.7, bf16[2048,128]{1,0:T(8,128)(2,1)} %bitcast.8, s32[4,16]{1,0:T(4,128)} %kept.1, s32[1]{0:T(128)S(6)} %copy.10.lengths, ...), custom_call_target="tpu_custom_call" | custom-call | tf_op jit(solution)/shard_map/pallas_call | solution.py:279
  34.3 2.0 %copy.11 = f32[128,1280]{1,0:T(8,128)} copy(f32[128,1280]{1,0:T(8,128)} %shard_map.82) | data formatting | bytes 1310720
where the time goes:
time: 36.9 us; the launch traced here: 36.2 us
  Pallas kernels  33.6 us (91%)
  local copies, waits for them, and re-layouts  1.97 us (5%)
  between operations  0.66 us (2%)
    pallas_call x1, Pallas kernels, body(): pl.pallas_call(functools.partial(kernel, n, heads), out_shape=jax.ShapeDt...  33.6 us
    unnamed x1, local copies, waits for them, and re-layouts  1.97 us

commit v1 on v0

--- a/solution.py
+++ b/solution.py
@@ -278,7 +278,7 @@
     dma = pltpu.SemaphoreType.DMA
     return pl.pallas_call(
         functools.partial(kernel, n, heads),
-        out_shape=jax.ShapeDtypeStruct((per_head * tokens, columns), f32),
+        out_shape=pltpu.VMEM((per_head * tokens, columns), f32),
         in_specs=[any_space] * 5 + [smem] * 2 + [any_space],
         out_specs=pl.BlockSpec(memory_space=pltpu.VMEM),
         scratch_shapes=[

time: 36.9 us -> 35 us (0.949)
  local copies, waits for them, and re-layouts: 1.97 us -> 0.84 us
  Pallas kernels: 33.6 us -> 32.8 us
    unnamed x1, local copies, waits for them, and re-layouts: 1.97 us -> 0.84 us
    pallas_call x1, Pallas kernels: 33.6 us -> 32.8 us  [body(): pl.pallas_call(functools.partial(kernel, n, heads), out_shape=pltpu.VMEM(...]
where the time goes in v1:
time: 35 us; the launch traced here: 34.3 us
  Pallas kernels  32.8 us (94%)
  local copies, waits for them, and re-layouts  0.84 us (2%)
  between operations  0.66 us (2%)
    pallas_call x1, Pallas kernels, body(): pl.pallas_call(functools.partial(kernel, n, heads), out_shape=pltpu.VMEM(...  32.8 us
    unnamed x1, local copies, waits for them, and re-layouts  0.84 us

profile of v1, /device:TPU:2, one launch (start us, length us, event | category | flops | bytes accessed | tf_op | source)
XLA Modules:
  0.0 34.3 jit_solution(14812507135833736431)
XLA Ops:
  0.7 32.8 %shard_map.82 = f32[128,1280]{1,0:T(8,128)S(1)} custom-call(bf16[64,640]{1,0:T(8,128)(2,1)} %bitcast.9, bf16[32,128,128]{2,1,0:T(8,128)(2,1)} %bitcast.5, bf16[32,128,128]{2,1,0:T(8,128)(2,1)} %bitcast.6, bf16[2048,128]{1,0:T(8,128)(2,1)} %bitcast.7, bf16[2048,128]{1,0:T(8,128)(2,1)} %bitcast.8, s32[4,16]{1,0:T(4,128)} %kept.1, s32[1]{0:T(128)S(6)} %copy.11.lengths, ...), custom_call_target="tpu_custom_call" | custom-call | tf_op jit(solution)/shard_map/pallas_call | solution.py:279
  33.4 0.8 %copy.10 = f32[128,1280]{1,0:T(8,128)} copy(f32[128,1280]{1,0:T(8,128)S(1)} %shard_map.82) | data formatting | bytes 1310720

commit v2 on v1

v2 whole, which is shorter than its diff:
```python
import functools
import math

import jax
import jax.numpy as jnp
from jax import lax
from jax.experimental import pallas as pl
from jax.experimental.pallas import tpu as pltpu
from jax.sharding import PartitionSpec as P

HD = 128
GQA = 5
BLOCK = 128
MOST = 8
CHUNK = MOST * BLOCK
SPLIT = 2

floor_value = -1e30
hidden_value = -3e30
factor = math.log2(math.e) / math.sqrt(HD)


def chosen_slots(kept, sample, base, blocks_here):
    slots = [jnp.int32(0)] * MOST
    count = jnp.int32(0)
    for e in range(kept.shape[1]):
        local = kept[sample, e] - base
        present = (local >= 0) & (local < blocks_here)
        rank = jnp.where(present, count, -1)
        slots = [jnp.where(rank == j, local, slots[j]) for j in range(MOST)]
        count = count + jnp.where(present, 1, 0)
    return slots, count


def rows_of(block):
    return jnp.concatenate([block[:, j * HD : (j + 1) * HD] for j in range(GQA)], axis=0)


def scores_of(asking, keys):
    return lax.dot_general(asking, keys, (((1,), (1,)), ((), ())), preferred_element_type=jnp.float32)


def softmax_part(scores, values):
    maximum = jnp.maximum(jnp.max(scores, axis=-1, keepdims=True), floor_value)
    weights = jnp.exp2((scores - maximum) * factor).astype(jnp.bfloat16)
    weight_sum = jnp.sum(weights.astype(jnp.float32), axis=-1, keepdims=True)
    return maximum, weight_sum, jnp.dot(weights, values, preferred_element_type=jnp.float32)


def low_bit(r):
    return r & -r


def lower_bits(r):
    return [bit for bit in (1 << k for k in reversed(range(16))) if bit < r]


def relay_order(n):
    return sorted((r for r in range(1, n) if low_bit(r) > 1), key=lambda r: (-low_bit(r), r))


def kernel(
    n, heads, prompts,
    q_hbm, pk_hbm, pv_hbm, sk_hbm, sv_hbm, kept, lengths, w_hbm,
    out,
    qbuf, pk, pv, sk, sv, wall, own_acc, own_max, own_sum, psend, pbuf, ssend, sbuf, att, fbuf, chosen,
    lsem, q_s, q_r, p_s, p_r, s_s, s_r, a_s, a_r, f_s, f_r, w_s, w_r, v_s, v_r,
):
    me = lax.axis_index("seq")
    head = lax.axis_index("head")
    prompt = lax.axis_index("prompt")
    tokens = q_hbm.shape[0]
    blocks_here = pk_hbm.shape[0]
    base = me * blocks_here
    per_head = n // heads
    piece = tokens // SPLIT

    def flipped(index, size, r):
        found, bit = 0, 1
        while bit < size:
            found = found + (index // bit + r // bit) % 2 * bit
            bit *= 2
        return found

    def partner(r):
        return flipped(me, n, r)

    def span(h):
        return pl.ds(h * piece, piece)

    loads = [
        pltpu.make_async_copy(src, dst, lsem.at[i])
        for i, (src, dst) in enumerate(
            ((q_hbm, qbuf.at[0]), (sk_hbm, sk), (sv_hbm, sv), (pk_hbm, pk), (pv_hbm, pv), (w_hbm, wall.at[head]))
        )
    ]
    for load in loads:
        load.start()

    barrier = pltpu.get_barrier_semaphore()
    for r in range(1, n):
        pl.semaphore_signal(barrier, inc=1, device_id={"seq": partner(r)})
    for r in range(1, heads):
        other = lax.rem(head + r, heads)
        pl.semaphore_signal(barrier, inc=1, device_id={"head": other})
        pl.semaphore_signal(barrier, inc=1, device_id={"head": other, "seq": partner(1)})
    for bit in lower_bits(prompts):
        pl.semaphore_signal(barrier, inc=1, device_id={"prompt": flipped(prompt, prompts, bit)})

    def choose(sample, carry):
        slots, count = chosen_slots(kept, sample, base, blocks_here)
        for j in range(MOST):
            chosen[sample, j] = slots[j]
        chosen[sample, MOST] = count
        return carry

    lax.fori_loop(0, n, choose, 0)
    pl.semaphore_wait(barrier, n - 1 + 2 * (heads - 1) + len(lower_bits(prompts)))

    def query_copy(r, h, low):
        return pltpu.make_async_remote_copy(
            qbuf.at[r - low, span(h)], qbuf.at[r, span(h)], q_s.at[r, h], q_r.at[r, h], device_id={"seq": partner(low)}
        )

    def part_copy(r, h):
        return pltpu.make_async_remote_copy(
            psend.at[r, span(h)], pbuf.at[r, span(h)], p_s.at[r, h], p_r.at[r, h], device_id={"seq": partner(r)}
        )

    def stat_copy(r, h):
        return pltpu.make_async_remote_copy(
            ssend.at[r, h], sbuf.at[r, h], s_s.at[r, h], s_r.at[r, h], device_id={"seq": partner(r)}
        )

    def attended_copy(r, h):
        low = low_bit(r)
        return pltpu.make_async_remote_copy(
            att.at[r - low, span(h)], att.at[r, span(h)], a_s.at[r, h], a_r.at[r, h], device_id={"seq": partner(low)}
        )

    def place_of(r):
        sample = partner(r)
        return sample // per_head, lax.rem(sample, per_head)

    def final_copy(r, h, across):
        reader, place = place_of(r)
        return pltpu.make_async_remote_copy(
            att.at[r, span(h)], fbuf.at[head, place, span(h)], f_s.at[r // 2, across, h], f_r.at[head, place, h],
            device_id={"head": reader, "seq": partner(1) if across else me},
        )

    def arrival(g, place, h):
        spot = fbuf.at[g, place, span(h)]
        return pltpu.make_async_remote_copy(
            spot, spot, f_s.at[0, 0, h], f_r.at[g, place, h], device_id={"seq": partner(1)}
        )

    def source(r):
        return lax.rem(head + heads - r, heads)

    share = w_hbm.shape[0] // (prompts * SPLIT)

    def weight_place(owner, k, c):
        return wall.at[owner, pl.ds((flipped(prompt, prompts, k) * SPLIT + c) * share, share)]

    def weight_copy(r, owner, c):
        place = weight_place(owner, 0, c)
        return pltpu.make_async_remote_copy(
            place, place, w_s.at[r, c], w_r.at[r, c], device_id={"head": lax.rem(head + r, heads)}
        )

    def spread_copy(r, k, c, sending):
        low = low_bit(k)
        place = weight_place(source(r), k - low if sending else k, c)
        return pltpu.make_async_remote_copy(
            place, place, v_s.at[r, k, c], v_r.at[r, k, c], device_id={"prompt": flipped(prompt, prompts, low)}
        )

    loads[0].wait()
    for h in range(SPLIT):
        for bit in lower_bits(n):
            query_copy(bit, h, bit).start()
    loads[5].wait()
    for c in range(SPLIT):
        for r in range(1, heads):
            weight_copy(r, head, c).start()

    def relay_queries(h):
        for r in relay_order(n):
            query_copy(r, h, low_bit(r)).wait_recv()
            for bit in lower_bits(low_bit(r)):
                query_copy(r + bit, h, bit).start()

    def spread_first(c):
        for r in range(1, heads):
            weight_copy(r, source(r), c).wait_recv()
            for bit in lower_bits(prompts):
                spread_copy(r, bit, c, True).start()

    def spread_rest(c):
        for r in range(1, heads):
            for k in relay_order(prompts):
                spread_copy(r, k, c, False).wait_recv()
                for bit in lower_bits(low_bit(k)):
                    spread_copy(r, k + bit, c, True).start()

    def spread_end(c):
        for r in range(1, heads):
            for k in range(1, prompts, 2):
                spread_copy(r, k, c, False).wait_recv()

    def prefix_part(asking, sample):
        keys = jnp.concatenate([pk[chosen[sample, j]] for j in range(MOST)], axis=0)
        values = jnp.concatenate([pv[chosen[sample, j]] for j in range(MOST)], axis=0)
        column = lax.broadcasted_iota(jnp.int32, (1, CHUNK), 1)
        hidden = jnp.where(column < chosen[sample, MOST] * BLOCK, 0.0, hidden_value)
        return softmax_part(scores_of(asking, keys) + hidden, values)

    asking = rows_of(qbuf[0])
    rows = asking.shape[0]
    last_seen = lengths[0] - tokens + lax.broadcasted_iota(jnp.int32, (rows, 1), 0) % tokens
    loads[1].wait()
    loads[2].wait()

    def own_scores(keys, start):
        column = start + lax.broadcasted_iota(jnp.int32, (1, keys.shape[0]), 1)
        return jnp.where(column <= last_seen, scores_of(asking, keys), hidden_value)

    def merged(one, two):
        maximum = jnp.maximum(one[0], two[0])
        shrink_one = jnp.exp2((one[0] - maximum) * factor)
        shrink_two = jnp.exp2((two[0] - maximum) * factor)
        return (
            maximum,
            one[1] * shrink_one + two[1] * shrink_two,
            one[2] * shrink_one + two[2] * shrink_two,
        )

    state = None
    for start in range(0, sk.shape[0], CHUNK):
        part = pl.ds(start, min(CHUNK, sk.shape[0] - start))
        latest = softmax_part(own_scores(sk[part], start), sv[part])
        state = latest if state is None else merged(state, latest)
    loads[3].wait()
    loads[4].wait()
    state = merged(state, prefix_part(asking, me))
    own_max[...] = jnp.broadcast_to(state[0], own_max.shape)
    own_sum[...] = jnp.broadcast_to(state[1], own_sum.shape)
    own_acc[...] = state[2]

    lane = lax.broadcasted_iota(jnp.int32, (piece, HD), 1)

    def remote_part(r, h):
        maximum, weight_sum, summed = prefix_part(rows_of(qbuf[r, span(h)]), partner(r))
        mean = (summed / jnp.maximum(weight_sum, 1e-30)).astype(jnp.bfloat16)
        top = jnp.zeros((piece, HD), jnp.float32)
        bottom = jnp.zeros((piece, HD), jnp.float32)
        for j in range(GQA):
            part = slice(j * piece, (j + 1) * piece)
            psend[r, span(h), j * HD : (j + 1) * HD] = mean[part]
            top = jnp.where(lane == j, maximum[part], top)
            bottom = jnp.where(lane == j, weight_sum[part], bottom)
        part_copy(r, h).start()
        square = jnp.concatenate([top, bottom, jnp.zeros((HD - 2 * piece, HD), jnp.float32)], axis=0)
        ssend[r, h] = square.T[: ssend.shape[2]]
        stat_copy(r, h).start()

    def odd_part(r, h):
        query_copy(r, h, 1).wait_recv()
        remote_part(r, h)

    relay_queries(0)
    for h in range(SPLIT):

        def even_step(i, carry):
            remote_part(2 * i + 2, h)
            return carry

        def odd_step(i, carry):
            odd_part(2 * i + 3, h)
            return carry

        lax.fori_loop(0, n // 2 - 1, even_step, 0)
        odd_part(1, h)
        if h + 1 < SPLIT:
            relay_queries(h + 1)
        lax.fori_loop(0, n // 2 - 1, odd_step, 0)
        spread_first(h)

    def stats_from(r, h):
        part_copy(r, h).wait_recv()
        stat_copy(r, h).wait_recv()
        padded = jnp.concatenate([sbuf[r, h], jnp.zeros((HD - sbuf.shape[2], HD), jnp.float32)], axis=0).T
        return padded[:piece], padded[piece : 2 * piece]

    def finish(r, h):
        reader, place = place_of(r)
        final_copy(r, h, 1).start()

        @pl.when(reader != head)
        def _():
            final_copy(r, h, 0).start()

        @pl.when(reader == head)
        def _():
            fbuf[head, place, span(h)] = att[r, span(h)]

    def merge_parts(h):
        stats = [stats_from(r, h) for r in range(1, n)]
        for j in range(GQA):
            part = pl.ds(j * tokens + h * piece, piece)
            columns = slice(j * HD, (j + 1) * HD)
            maximum = own_max[part]
            for top, _ in stats:
                maximum = jnp.maximum(maximum, top[:, j : j + 1])
            scale = jnp.exp2((own_max[part] - maximum) * factor)
            total = own_acc[part] * scale
            weight_sum = own_sum[part] * scale
            for r, (top, bottom) in zip(range(1, n), stats):
                portion = jnp.exp2((top[:, j : j + 1] - maximum) * factor) * bottom[:, j : j + 1]
                total = total + portion * pbuf[r, span(h), columns].astype(jnp.float32)
                weight_sum = weight_sum + portion
            att[0, span(h), columns] = (total / weight_sum).astype(jnp.bfloat16)
        for bit in lower_bits(n):
            if bit > 1:
                attended_copy(bit, h).start()
        finish(0, h)

    def relay_attended(h):
        for r in relay_order(n):
            attended_copy(r, h).wait_recv()
            for bit in lower_bits(low_bit(r)):
                if bit > 1:
                    attended_copy(r + bit, h).start()
            finish(r, h)

    def is_local(g, place):
        return (g == head) & ((head * per_head + place) % 2 == me % 2)

    def project(h):
        total = None
        for g in range(heads):
            for place in range(per_head):

                @pl.when(jnp.logical_not(is_local(g, place)))
                def _():
                    arrival(g, place, h).wait_recv()

        for g in range(heads):
            block = fbuf[g, :, span(h)].reshape(per_head * piece, fbuf.shape[-1])
            term = jnp.dot(block, wall[g], preferred_element_type=jnp.float32)
            total = term if total is None else total + term
        for place in range(per_head):
            out[pl.ds(place * tokens + h * piece, piece)] = total[place * piece : (place + 1) * piece]

    for h in range(SPLIT):
        merge_parts(h)
        spread_rest(h)
    for h in range(SPLIT):
        relay_attended(h)
    for c in range(SPLIT):
        spread_end(c)
    for h in range(SPLIT):
        project(h)

    for h in range(SPLIT):
        for r in range(1, n):
            query_copy(r, h, low_bit(r)).wait_send()
            part_copy(r, h).wait_send()
            stat_copy(r, h).wait_send()
        for r in range(0, n, 2):
            if r:
                attended_copy(r, h).wait_send()
            final_copy(r, h, 1).wait_send()

            @pl.when(place_of(r)[0] != head)
            def _():
                final_copy(r, h, 0).wait_send()

        for r in range(1, heads):
            weight_copy(r, head, h).wait_send()
            for k in range(1, prompts):
                spread_copy(r, k, h, True).wait_send()


def body(n, heads, prompts, queries, prefix_keys, prefix_values, suffix_keys, suffix_values, kept_blocks, suffix_lengths, out_weight):
    tokens, width = queries.shape[1:]
    blocks_here = prefix_keys.shape[0] // BLOCK
    slots = suffix_keys.shape[1]
    columns = out_weight.shape[1]
    per_head = n // heads
    assert prefix_keys.shape[1] == HD and width == GQA * HD and n % heads == 0
    assert n & (n - 1) == 0 and prompts & (prompts - 1) == 0 and per_head % 2 == 0
    bf16, f32 = jnp.bfloat16, jnp.float32
    any_space = pl.BlockSpec(memory_space=pltpu.HBM)
    smem = pl.BlockSpec(memory_space=pltpu.SMEM)
    dma = pltpu.SemaphoreType.DMA
    return pl.pallas_call(
        functools.partial(kernel, n, heads, prompts),
        out_shape=pltpu.VMEM((per_head * tokens, columns), f32),
        in_specs=[any_space] * 5 + [smem] * 2 + [any_space],
        out_specs=pl.BlockSpec(memory_space=pltpu.VMEM),
        scratch_shapes=[
            pltpu.VMEM((n, tokens, width), bf16),
            pltpu.VMEM((blocks_here, BLOCK, HD), bf16),
            pltpu.VMEM((blocks_here, BLOCK, HD), bf16),
            pltpu.VMEM((slots, HD), bf16),
            pltpu.VMEM((slots, HD), bf16),
            pltpu.VMEM((heads,) + out_weight.shape, bf16),
            pltpu.VMEM((GQA * tokens, HD), f32),
            pltpu.VMEM((GQA * tokens, HD), f32),
            pltpu.VMEM((GQA * tokens, HD), f32),
            pltpu.VMEM((n, tokens, width), bf16),
            pltpu.VMEM((n, tokens, width), bf16),
            pltpu.VMEM((n, SPLIT, 8, HD), f32),
            pltpu.VMEM((n, SPLIT, 8, HD), f32),
            pltpu.VMEM((n, tokens, width), bf16),
            pltpu.VMEM((heads, per_head, tokens, width), bf16),
            pltpu.SMEM((n, MOST + 1), jnp.int32),
            dma((6,)),
            dma((n, SPLIT)), dma((n, SPLIT)),
            dma((n, SPLIT)), dma((n, SPLIT)),
            dma((n, SPLIT)), dma((n, SPLIT)),
            dma((n, SPLIT)), dma((n, SPLIT)),
            dma((n // 2, 2, SPLIT)), dma((heads, per_head, SPLIT)),
            dma((heads, SPLIT)), dma((heads, SPLIT)),
            dma((heads, prompts, SPLIT)), dma((heads, prompts, SPLIT)),
        ],
        compiler_params=pltpu.CompilerParams(
            collective_id=0, has_side_effects=True, vmem_limit_bytes=63 * 1024 * 1024
        ),
    )(
        queries[0],
        prefix_keys.reshape(blocks_here, BLOCK, HD),
        prefix_values.reshape(blocks_here, BLOCK, HD),
        suffix_keys[0],
        suffix_values[0],
        kept_blocks,
        suffix_lengths,
        out_weight,
    )


def solution(mesh):
    in_specs = (
        P(("prompt", "seq"), None, "head"),
        P(("prompt", "seq"), "head"),
        P(("prompt", "seq"), "head"),
        P(("prompt", "seq"), None, "head"),
        P(("prompt", "seq"), None, "head"),
        P("prompt", None),
        P(("prompt", "seq")),
        P("head", "seq"),
    )
    out_specs = P(("prompt", "head"), "seq")
    part = functools.partial(body, mesh.shape["seq"], mesh.shape["head"], mesh.shape["prompt"])
    return jax.shard_map(part, mesh=mesh, in_specs=in_specs, out_specs=out_specs, check_vma=False)
```

time: 35 us -> 30.6 us (0.87); the launches traced: 34.3 us -> 30.4 us
  Pallas kernels: 32.8 us -> 28.9 us
    pallas_call x1, Pallas kernels: 32.8 us -> 28.9 us  [body(): pl.pallas_call(functools.partial(kernel, n, heads, prompts), out_shape=pl...]
where the time goes in v2:
time: 30.6 us; the launch traced here: 30.4 us
  Pallas kernels  28.9 us (94%)
  local copies, waits for them, and re-layouts  0.84 us (3%)
  between operations  0.66 us (2%)
    pallas_call x1, Pallas kernels, body(): pl.pallas_call(functools.partial(kernel, n, heads, prompts), out_shape=pl...  28.9 us
    unnamed x1, local copies, waits for them, and re-layouts  0.84 us

profile of v2, /device:TPU:2, one launch (start us, length us, event | category | flops | bytes accessed | tf_op | source)
XLA Modules:
  0.0 30.4 jit_solution(4411822811567456111)
XLA Ops:
  0.7 28.9 %shard_map.82 = f32[128,1280]{1,0:T(8,128)S(1)} custom-call(bf16[64,640]{1,0:T(8,128)(2,1)} %bitcast.9, bf16[32,128,128]{2,1,0:T(8,128)(2,1)} %bitcast.5, bf16[32,128,128]{2,1,0:T(8,128)(2,1)} %bitcast.6, bf16[2048,128]{1,0:T(8,128)(2,1)} %bitcast.7, bf16[2048,128]{1,0:T(8,128)(2,1)} %bitcast.8, s32[4,16]{1,0:T(4,128)} %kept.1, s32[1]{0:T(128)S(6)} %copy.11.lengths, ...), custom_call_target="tpu_custom_call" | custom-call | tf_op jit(solution)/shard_map/pallas_call | solution.py:398
  29.6 0.8 %copy.10 = f32[128,1280]{1,0:T(8,128)} copy(f32[128,1280]{1,0:T(8,128)S(1)} %shard_map.82) | data formatting | bytes 1310720
